TPU v7x, 512 devices: a 4x2x32 block of a 4x8x32 slice. The times are simulated.
512 devices in a mesh: group: 2 (over y), seq: 128 (over z, x), tensor: 2 (over core).
Axes of the slice: x: 4, y: 2, z: 32, core: 2. Of those that a mesh axis runs over, the one named last changes fastest.
The devices are a block of a 4x8x32 slice.
Arguments:
- queries: bfloat16 [64, 64, 128], P('group', 'tensor'), parts along dimension 0, may hold values from -10 to 10
- k_cache: bfloat16 [2048, 8, 128, 128], P(('group', 'seq'), 'tensor'), parts along dimension 0, may hold values from -6 to 6
- value_cache: bfloat16 [2048, 8, 128, 128], P(('group', 'seq'), 'tensor'), parts along dimension 0, may hold values from -6 to 6
- kv_lengths: int32 [64], P('group'), parts along dimension 0, may hold values from 1 to 32768, as said below
- page_table: int32 [64, 256], P('group'), parts along dimension 0, may hold values from -1 to 1023, as said below
- request_batch_row: int32 [64], P('group'), parts along dimension 0, may hold values from 0 to 31, each once
Outputs:
- attended: bfloat16 [64, 64, 128], P('group', 'tensor'), parts along dimension 0
There are 2 independent parts, one for each index of `group`. A program takes and returns all parts, laid end to end along the dimension named above; each array names one. Nothing has to cross between parts.
Inputs may be any that keep to these rules, and one draw needn't show every extreme that they name: `kv_lengths`: the longest request holds exactly 32768 tokens. `page_table`: row r lists in order the cache slots of the first ceil(kv_lengths[r] / 128) pages of request r and -1 after them; no slot is listed twice.
All inputs are finite; a program needn't handle non-finite values.
Results may differ from a plain program's by a relative error of at most 0.0042.
Values may be sent and summed in bfloat16 or wider, within the bound.
No kernel may reach another device: no remote copies, remote signals or barrier semaphores. Data moves between devices by JAX's collectives and lax.ppermute only.
A program may use at most 64 MiB of HBM per device.

v0:
```python
import functools

import jax
import jax.numpy as jnp
from jax import lax
from jax.sharding import Mesh
from jax.sharding import PartitionSpec as P

SEQ = ("seq_0", "seq_1")
GROUP_SEQ = ("group", "seq_0", "seq_1")


NEG_BIG = -1e30


def one_axis_at_a_time(x, axes):
    return functools.reduce(lax.pmax, axes, x)


def sum_by_axis(x, axes, dim):
    for axis in axes:
        x = lax.psum_scatter(x, axis, scatter_dimension=dim, tiled=True)
    return x


def laid_out(pieces, dim):
    pieces = jnp.moveaxis(pieces, 0, dim)
    shape = pieces.shape
    return pieces.reshape(*shape[:dim], shape[dim] * shape[dim + 1], *shape[dim + 2 :])


def gather_in_order(x, axes, turns):
    pieces = x
    for k in turns:
        pieces = lax.all_gather(pieces, axes[k])
    done = turns[::-1]
    back = [done.index(k) for k in range(len(axes))]
    pieces = pieces.transpose(*back, *range(len(axes), pieces.ndim))
    return pieces.reshape(-1, *x.shape)


def whole_of(x, axes, turns, dim):
    return laid_out(gather_in_order(x, axes, turns), dim)


def slot_owners(page_table, first_slot, slot_count):
    global_ids = first_slot + jnp.arange(slot_count, dtype=jnp.int32)
    match_int = (page_table[None, :, :] == global_ids[:, None, None]).astype(jnp.int32)
    request_ids = jnp.arange(page_table.shape[0], dtype=jnp.int32)
    page_ids = jnp.arange(page_table.shape[1], dtype=jnp.int32)
    owner_ids = jnp.sum(match_int * request_ids[None, :, None], axis=(1, 2))
    logical = jnp.sum(match_int * page_ids[None, None, :], axis=(1, 2))
    live_mask = jnp.sum(match_int, axis=(1, 2)) > 0
    return (owner_ids, logical, live_mask)


def page_partials(q_rows, key_pages, value_pages, owner_ids, logical, live_mask, kv_lengths):
    slot_count, heads_kv, page_len, head_dim = key_pages.shape
    group_width = q_rows.shape[1] // heads_kv
    slot_queries = jnp.take(q_rows, owner_ids, axis=0).reshape(
        slot_count, heads_kv, group_width, head_dim
    )
    scores = jnp.einsum(
        "skgd,sktd->skgt", slot_queries, key_pages, preferred_element_type=jnp.float32
    ) * head_dim ** (-0.5)
    positions = logical[:, None] * page_len + jnp.arange(page_len, dtype=jnp.int32)[None, :]
    valid_mask = live_mask[:, None] & (positions < jnp.take(kv_lengths, owner_ids)[:, None])
    valid_wide = valid_mask[:, None, None, :]
    masked = jnp.where(valid_wide, scores, NEG_BIG)
    page_max = jnp.max(masked, axis=3)
    weights = jnp.where(valid_wide, jnp.exp(masked - page_max[..., None]), 0.0)
    page_sum = jnp.sum(weights, axis=3)
    page_out = jnp.einsum(
        "skgt,sktd->skgd",
        weights.astype(jnp.bfloat16),
        value_pages,
        preferred_element_type=jnp.float32,
    )
    return (
        page_max.reshape(slot_count, -1),
        page_sum.reshape(slot_count, -1),
        page_out.reshape(slot_count, -1),
    )


def request_partials(page_max, page_sum, page_out, owner_ids, live_mask, requests, head_dim):
    slot_count, heads_local = page_max.shape
    owned = (owner_ids[:, None] == jnp.arange(requests, dtype=jnp.int32)[None, :]) & live_mask[
        :, None
    ]
    req_max = jnp.max(jnp.where(owned[:, :, None], page_max[:, None, :], NEG_BIG), axis=0)
    factor = jnp.where(
        live_mask[:, None], jnp.exp(page_max - jnp.take(req_max, owner_ids, axis=0)), 0.0
    )
    owned_float = owned.astype(jnp.float32)
    req_sum = jnp.einsum(
        "sr,sh->rh", owned_float, page_sum * factor, precision=lax.Precision.HIGHEST
    )
    scaled = (page_out.reshape(slot_count, heads_local, head_dim) * factor[..., None]).reshape(
        slot_count, -1
    )
    req_out = jnp.einsum("sr,sx->rx", owned_float, scaled, precision=lax.Precision.HIGHEST)
    return (req_max, req_sum, req_out.reshape(requests, heads_local, head_dim))


def shards(queries, k_cache, value_cache, kv_lengths, page_table, request_batch_row):
    slot_count = k_cache.shape[0]
    requests = queries.shape[0]
    heads_local = queries.shape[1]
    head_dim = queries.shape[2]
    first_slot = lax.axis_index(SEQ) * slot_count
    owner_ids, logical, live_mask = slot_owners(page_table, first_slot, slot_count)
    q_rows = jnp.take(queries, request_batch_row, axis=0)
    page_max, page_sum, page_out = page_partials(
        q_rows, k_cache, value_cache, owner_ids, logical, live_mask, kv_lengths
    )
    owner_used, live_used = (owner_ids, live_mask)
    req_max, req_sum, req_out = request_partials(
        page_max, page_sum, page_out, owner_used, live_used, requests, head_dim
    )
    overall = one_axis_at_a_time(req_max, SEQ)
    factor = jnp.exp(req_max - overall)
    flat_sum = (req_sum * factor).reshape(-1)
    flat_out = (req_out * factor[..., None]).reshape(requests * heads_local, head_dim)
    part_out, part_sum = (sum_by_axis(flat_out, SEQ, 0), sum_by_axis(flat_sum, SEQ, 0))
    finished = (part_out / part_sum[:, None]).astype(jnp.bfloat16)
    result = whole_of(finished, SEQ, (0, 1), 0).reshape(requests, heads_local, head_dim)
    return jnp.zeros_like(queries).at[request_batch_row].set(result)


def solution(mesh):
    finer = Mesh(
        mesh.devices.reshape(mesh.shape["group"], 32, 4, mesh.shape["tensor"]),
        ("group", "seq_0", "seq_1", "tensor"),
    )
    placed = (
        P("group", "tensor", None),
        P(GROUP_SEQ, "tensor", None, None),
        P(GROUP_SEQ, "tensor", None, None),
        P("group"),
        P("group", None),
        P("group"),
    )
    return jax.shard_map(
        shards, mesh=finer, in_specs=placed, out_specs=P("group", "tensor", None), check_vma=False
    )
```

profile of v0, /device:TPU:40, one launch (start us, length us, event | category | flops | bytes accessed | tf_op | source)
XLA Modules:
  0.0 388.7 jit_solution(14386119310870982077)
XLA Ops:
  6.6 0.7 copy-done.4
  7.3 1.4 fusion.2
  8.7 0.6 copy-done.1
  9.4 0.6 gather_fusion
  10.0 0.3 copy-done.3
  10.3 0.6 gather_fusion.1
  11.1 0.6 gather_fusion.2
  11.8 0.8 fusion.27
  12.8 0.6 gather_fusion.3
  13.3 147.4 %pmax.14 = f32[32,32]{1,0:T(8,128)S(1)} all-reduce(f32[32,32]{1,0:T(8,128)S(1)} %select_reduce_fusion), channel_id=1, replica_groups=mesh['group'=2,'seq_0'=32,'seq_1'=4,'tensor'=2] {'seq_0'}, use_global_device_ids=true, to_apply=%region_5.6 | all-reduce | flops 1024 | bytes 8192 | tf_op jit(solution)/shard_map/pmax | solution.py:17
  160.7 17.4 %pmax.15 = f32[32,32]{1,0:T(8,128)S(1)} all-reduce(f32[32,32]{1,0:T(8,128)S(1)} %pmax.14), channel_id=1, replica_groups=mesh['group'=2,'seq_0'=32,'seq_1'=4,'tensor'=2] {'seq_1'}, use_global_device_ids=true, to_apply=%region_6.7 | all-reduce | flops 1024 | bytes 8192 | tf_op jit(solution)/shard_map/pmax | solution.py:17
  178.3 0.4 convolution_bitcast_fusion
  178.7 0.5 convolution_multiply_fusion
  179.2 1.1 copy.22
  180.7 0.3 convolution_multiply_fusion.2
  181.0 1.3 dynamic-slice.2
  182.3 1.3 dynamic-slice
  184.2 52.9 %all-reduce.1 = f32[1024]{0:T(1024)S(1)} all-reduce(f32[1024]{0:T(1024)S(1)} %reshape.182), channel_id=6, replica_groups=mesh['group'=2,'seq_0'=32,'seq_1'=4,'tensor'=2] {'seq_0'}, use_global_device_ids=true, to_apply=%region_10.11.clone | all-reduce | flops 1024 | bytes 8192
  237.8 57.2 %reduce-scatter.2.cloned.1.call-done = f32[32,128]{1,0:T(8,128)} async-done(((f32[1024,128]{1,0:T(8,128)}), f32[32,128]{1,0:T(8,128)}) %reduce-scatter.2.cloned.1.call-update) | async-done | bytes 16400 | tf_op jit(solution)/shard_map/reduce_scatter | solution.py:22
  295.0 17.0 %all-reduce.3 = (f32[32,128]{1,0:T(8,128)S(1)}, f32[32]{0:T(128)S(1)}) all-reduce(f32[32,128]{1,0:T(8,128)} %reduce-scatter.2.cloned.1.call-done, f32[32]{0:T(128)S(1)} %dynamic-slice.3), channel_id=5, replica_groups=mesh['group'=2,'seq_0'=32,'seq_1'=4,'tensor'=2] {'seq_1'}, use_global_device_ids=true, to_apply=%region_8.9.clone | all-reduce | flops 4128 | bytes 33024
  312.1 52.9 %all-gather = bf16[256,128]{1,0:T(8,128)(2,1)S(1)} all-gather(bf16[8,128]{1,0:T(8,128)(2,1)S(1)} %fusion.17), channel_id=2, replica_groups=mesh['group'=2,'seq_0'=32,'seq_1'=4,'tensor'=2] {'seq_0'}, dimensions={0}, use_global_device_ids=true | all-gather | bytes 67584 | tf_op jit(solution)/shard_map/all_gather | solution.py:35
  364.9 12.3 %all-gather.1 = bf16[128,8,128]{2,1,0:T(8,128)(2,1)S(1)} all-gather(bf16[32,8,128]{2,1,0:T(8,128)(2,1)S(1)} %bitcast.45), channel_id=3, replica_groups=mesh['group'=2,'seq_0'=32,'seq_1'=4,'tensor'=2] {'seq_1'}, dimensions={0}, use_global_device_ids=true | all-gather | bytes 327680 | tf_op jit(solution)/shard_map/all_gather | solution.py:35
  377.3 0.7 broadcast_in_dim.104
  378.0 3.9 scatter_fusion
  (33 shorter events, 1.5 us)
Async XLA Ops:
  6.5 5.2 %copy-start = (bf16[8,4,128,128]{3,2,1,0:T(8,128)(2,1)S(1)}, bf16[8,4,128,128]{3,2,1,0:T(8,128)(2,1)}, u32[]{:S(2)}) copy-start(bf16[8,4,128,128]{3,2,1,0:T(8,128)(2,1)} %param.7) | copy-start | bytes 3145732
  6.6 0.7 copy-start.4
  6.6 288.4 %reduce-scatter.2.cloned.1.call-start = ((), (), s32[]{:S(2)}) async-start(), calls=%async_computation.1 | async-start | bytes 540672 | tf_op jit(solution)/shard_map/reduce_scatter | solution.py:22
  8.7 0.7 copy-start.1
  9.4 0.9 copy-start.3
  10.9 167.3 %copy-start.2 = (bf16[8,4,128,128]{3,2,1,0:T(8,128)(2,1)S(1)}, bf16[8,4,128,128]{3,2,1,0:T(8,128)(2,1)}, u32[]{:S(2)}) copy-start(bf16[8,4,128,128]{3,2,1,0:T(8,128)(2,1)} %param.8) | copy-start | bytes 3145732
Sparse Core Ops, SparseCore 0:
  180.5 114.4 reduce-scatter.1
where the time goes:
time: 389 us
  blocking collectives  300 us (77%)
  waiting for transfers between devices  57.2 us (15%)
  between operations  14.8 us (4%)
  local copies, waits for them, and re-layouts  12.8 us (3%)
    pmax x2, blocking collectives, one_axis_at_a_time(): return functools.reduce(lax.pmax, axes, x)  165 us
    unnamed x2, blocking collectives  69.9 us
    all_gather x2, blocking collectives, gather_in_order(): pieces = lax.all_gather(pieces, axes[k])  65.2 us
    reduce_scatter x1, waiting for transfers between devices, sum_by_axis(): x = lax.psum_scatter(x, axis, scatter_dimension=dim, tiled=True)  57.2 us
  transfers between devices with their start and end apart: 1, of which 1 were waited for; matrix products, arithmetic and copies ran while one was open for 1% of the time, Pallas kernels for 0%

commit v1 on v0

v1 whole, which is shorter than its diff:
```python
import functools

import jax
import jax.numpy as jnp
from jax import lax
from jax.experimental import pallas as pl
from jax.experimental.pallas import tpu as pltpu
from jax.sharding import Mesh
from jax.sharding import PartitionSpec as P

NEG_BIG = -1e30
SIDE = 4
BLOCK = ("near", "across")
SEQ = ("far", "near", "across")
GROUP_SEQ = ("group", "far", "near", "across")
STAT_ROWS = 8
STAT_ROWS_BF = 16


def attend_kernel(
    place, batch_row, lengths, table, queries, k_hbm, v_hbm, out, k_buf, v_buf, rows, stats, sems
):
    slots, heads_kv, page_len, width = k_buf.shape
    heads = queries.shape[1]
    group = heads // heads_kv
    peers = out.shape[0]
    share = heads // peers
    max_pages = table.shape[1]

    def k_copy(s):
        return pltpu.make_async_copy(k_hbm.at[s], k_buf.at[s], sems.at[0, s])

    def v_copy(s):
        return pltpu.make_async_copy(v_hbm.at[s], v_buf.at[s], sems.at[1, s])

    for s in range(slots):
        k_copy(s).start()
    for s in range(slots):
        v_copy(s).start()

    first_slot = place[0]
    first_lane = place[1]
    lane = lax.broadcasted_iota(jnp.int32, (heads, page_len), 1)
    entry = table[...]
    code = (
        lax.broadcasted_iota(jnp.int32, entry.shape, 0) * max_pages
        + lax.broadcasted_iota(jnp.int32, entry.shape, 1)
        + 1
    ).astype(jnp.float32)
    owner_row = jnp.zeros((STAT_ROWS // 2, page_len), jnp.float32)
    slot_queries = []
    valid_count = []
    for s in range(slots):
        found = jnp.max(jnp.where(entry == first_slot + s, code, 0.0)).astype(jnp.int32)
        index = jnp.maximum(found - 1, 0)
        request = index // max_pages
        page = index % max_pages
        row = batch_row[request]
        left = jnp.where(found > 0, lengths[request] - page * page_len, 0)
        valid_count.append(left)
        slot_queries.append(row)
        marked = jnp.where(found > 0, row + 1, 0).astype(jnp.float32)
        owner_row = jnp.where(
            lane[: STAT_ROWS // 2] == first_lane + s, marked, owner_row
        )

    scale = width ** (-0.5)
    max_rows = jnp.zeros((heads, page_len), jnp.float32)
    sum_rows = jnp.zeros((heads, page_len), jnp.float32)
    weights = []
    for s in range(slots):
        k_copy(s).wait()
        q = queries[slot_queries[s]]
        parts = []
        for k in range(heads_kv):
            full = lax.dot_general(
                q, k_buf[s, k], (((1,), (1,)), ((), ())), preferred_element_type=jnp.float32
            )
            parts.append(full[k * group : (k + 1) * group])
        valid = lane < valid_count[s]
        scores = jnp.where(valid, jnp.concatenate(parts, axis=0) * scale, NEG_BIG)
        top = jnp.max(scores, axis=1, keepdims=True)
        weight = jnp.where(valid, jnp.exp(scores - top), 0.0)
        total = jnp.sum(weight, axis=1, keepdims=True)
        mine = lane == first_lane + s
        max_rows = jnp.where(mine, top, max_rows)
        sum_rows = jnp.where(mine, total, sum_rows)
        weights.append(weight.astype(jnp.bfloat16))
    for s in range(slots):
        v_copy(s).wait()
        for k in range(heads_kv):
            full = jnp.dot(weights[s], v_buf[s, k], preferred_element_type=jnp.float32)
            rows[s * heads + k * group : s * heads + (k + 1) * group] = full[
                k * group : (k + 1) * group
            ]
    stats[:heads] = max_rows
    stats[heads:] = sum_rows
    for p in range(peers):
        for h in range(share):
            out[p, h * slots : (h + 1) * slots] = rows[pl.ds(p * share + h, slots, stride=heads)]
        first = p * share
        out[p, share * slots :] = jnp.concatenate(
            [stats[first : first + share], stats[heads + first : heads + first + share], owner_row],
            axis=0,
        )


def pieces_of(x):
    high = x.astype(jnp.bfloat16).astype(jnp.float32)
    rest = x - high
    middle = rest.astype(jnp.bfloat16).astype(jnp.float32)
    return high, middle, rest - middle


def merge_slots_kernel(got, out):
    peers, height, width = got.shape
    blocks, out_height, _ = out.shape
    slots = (height - STAT_ROWS) // 2
    share = 2
    requests = (out_height - STAT_ROWS_BF) // share
    stat = got[0, share * slots :]
    for i in range(1, peers):
        stat = stat + got[i, share * slots :]
    owner = stat[2 * share : 2 * share + 1].astype(jnp.int32) - 1
    owned = owner == lax.broadcasted_iota(jnp.int32, (requests, width), 0)
    tops = []
    totals = []
    for h in range(share):
        data = got[:, h * slots : (h + 1) * slots].reshape(peers * slots, width)
        slot_top = stat[h : h + 1]
        top = jnp.max(jnp.where(owned, slot_top, NEG_BIG), axis=1, keepdims=True)
        factor = jnp.where(owned, jnp.exp(slot_top - top), 0.0)
        total = jnp.sum(factor * stat[share + h : share + h + 1], axis=1, keepdims=True)
        merged = jnp.dot(
            factor, data, precision=lax.Precision.HIGHEST, preferred_element_type=jnp.float32
        )
        scaled = jnp.where(total > 0.0, merged / jnp.where(total > 0.0, total, 1.0), 0.0)
        scaled = scaled.astype(jnp.bfloat16)
        for j in range(blocks):
            out[j, h * requests : (h + 1) * requests] = scaled
        tops.append(top)
        totals.append(total)
    lane = lax.broadcasted_iota(jnp.int32, (share * requests, width), 1)
    table = jnp.zeros((share * requests, width), jnp.float32)
    columns = zip(
        pieces_of(jnp.concatenate(tops, axis=0)), pieces_of(jnp.concatenate(totals, axis=0))
    )
    for n, (top, total) in enumerate(columns):
        table = jnp.where(lane == 2 * n, top, table)
        table = jnp.where(lane == 2 * n + 1, total, table)
    square = jnp.concatenate(
        [table, jnp.zeros((width - share * requests, width), jnp.float32)], axis=0
    )
    tile = jnp.transpose(square)[:STAT_ROWS_BF].astype(jnp.bfloat16)
    for j in range(blocks):
        out[j, share * requests :] = tile


def merge_blocks_kernel(got, out):
    blocks, height, width = got.shape
    peers = out.shape[0]
    count = height - STAT_ROWS_BF
    tops = []
    totals = []
    for j in range(blocks):
        tile = got[j, count:].astype(jnp.float32)
        tops.append(tile[0:1] + tile[2:3] + tile[4:5])
        totals.append(tile[1:2] + tile[3:4] + tile[5:6])
    top = jnp.concatenate(tops, axis=0)
    total = jnp.concatenate(totals, axis=0)
    share = jnp.exp(top - jnp.max(top, axis=0, keepdims=True)) * total
    whole = jnp.sum(share, axis=0, keepdims=True)
    share = jnp.where(whole > 0.0, share / jnp.where(whole > 0.0, whole, 1.0), 0.0)
    square = jnp.concatenate([share, jnp.zeros((width - blocks, width), jnp.float32)], axis=0)
    column = jnp.transpose(square)[:count]
    result = column[:, 0:1] * got[0, :count].astype(jnp.float32)
    for j in range(1, blocks):
        result = result + column[:, j : j + 1] * got[j, :count].astype(jnp.float32)
    result = result.astype(jnp.bfloat16)
    for p in range(peers):
        out[p] = result


def in_vmem():
    return pl.BlockSpec(memory_space=pltpu.VMEM)


def in_smem():
    return pl.BlockSpec(memory_space=pltpu.SMEM)


def shards(blocks, queries, k_cache, value_cache, kv_lengths, page_table, request_batch_row):
    slots, heads_kv, page_len, width = k_cache.shape
    requests, heads, _ = queries.shape
    peers = SIDE * SIDE
    share = heads // peers
    place = jnp.stack(
        [lax.axis_index(SEQ) * slots, lax.axis_index(BLOCK) * slots]
    ).astype(jnp.int32)
    partial = pl.pallas_call(
        attend_kernel,
        out_shape=jax.ShapeDtypeStruct((peers, share * slots + STAT_ROWS, width), jnp.float32),
        in_specs=[in_smem(), in_smem(), in_smem(), in_vmem(), in_vmem()]
        + [pl.BlockSpec(memory_space=pl.ANY)] * 2,
        out_specs=in_vmem(),
        scratch_shapes=[
            pltpu.VMEM(k_cache.shape, k_cache.dtype),
            pltpu.VMEM(value_cache.shape, value_cache.dtype),
            pltpu.VMEM((slots * heads, width), jnp.float32),
            pltpu.VMEM((2 * heads, page_len), jnp.float32),
            pltpu.SemaphoreType.DMA((2, slots)),
        ],
        name="attend",
    )(place, request_batch_row, kv_lengths, page_table, queries, k_cache, value_cache)
    partial = lax.all_to_all(partial, BLOCK, 0, 0)
    merged = pl.pallas_call(
        merge_slots_kernel,
        out_shape=jax.ShapeDtypeStruct(
            (blocks, share * requests + STAT_ROWS_BF, width), jnp.bfloat16
        ),
        in_specs=[in_vmem()],
        out_specs=in_vmem(),
        name="merge_slots",
    )(partial)
    merged = lax.all_to_all(merged, "far", 0, 0)
    finished = pl.pallas_call(
        merge_blocks_kernel,
        out_shape=jax.ShapeDtypeStruct((peers, share * requests, width), jnp.bfloat16),
        in_specs=[in_vmem()],
        out_specs=in_vmem(),
        name="merge_blocks",
    )(merged)
    finished = lax.all_to_all(finished, BLOCK, 0, 0)
    return finished.reshape(heads, requests, width).transpose(1, 0, 2)


def solution(mesh):
    blocks = mesh.shape["seq"] // (SIDE * SIDE)
    finer = Mesh(
        mesh.devices.reshape(mesh.shape["group"], blocks, SIDE, SIDE, mesh.shape["tensor"]),
        ("group", "far", "near", "across", "tensor"),
    )
    placed = (
        P("group", "tensor", None),
        P(GROUP_SEQ, "tensor", None, None),
        P(GROUP_SEQ, "tensor", None, None),
        P("group"),
        P("group", None),
        P("group"),
    )
    return jax.shard_map(
        functools.partial(shards, blocks),
        mesh=finer,
        in_specs=placed,
        out_specs=P("group", "tensor", None),
        check_vma=False,
    )
```

time: 389 us -> 119 us (0.31)
  blocking collectives: 300 us -> 106 us
  waiting for transfers between devices: 57.2 us -> 0 us
  between operations: 14.8 us -> 0.01 us
  local copies, waits for them, and re-layouts: 12.8 us -> 0.81 us
  Pallas kernels: 0 us -> 10.6 us
    pmax x2 -> x0, blocking collectives: 165 us -> none  [one_axis_at_a_time(): return functools.reduce(lax.pmax, axes, x)]
    all_to_all x0 -> x3, blocking collectives: none -> 106 us  [the longest x1 71.4 us: shards(): merged = lax.all_to_all(merged, 'far', 0, 0)]
    unnamed x2 -> x0, blocking collectives: 69.9 us -> none
    all_gather x2 -> x0, blocking collectives: 65.2 us -> none  [gather_in_order(): pieces = lax.all_gather(pieces, axes[k])]
    reduce_scatter x1 -> x0, waiting for transfers between devices: 57.2 us -> none  [sum_by_axis(): x = lax.psum_scatter(x, axis, scatter_dimension=dim, tiled=True)]
    pallas_call x0 -> x3, Pallas kernels: none -> 10.6 us  [the longest x1 6.69 us: shards(): pl.pallas_call(attend_kernel, out_shape=jax.ShapeDtypeStruct((peers, shar...]
    unnamed x14 -> x0, local copies, waits for them, and re-layouts: 4.37 us -> none
  transfers between devices with their start and end apart: 1 -> 0, of which waited for: 1 -> 0; matrix products, arithmetic and copies ran while one was open for 1% -> 0% of each run, Pallas kernels for 0% -> 0%
where the time goes in v1:
time: 119 us; the launch traced here: 118 us
  blocking collectives  106 us (89%)
  Pallas kernels  10.6 us (9%)
    all_to_all x1, blocking collectives, shards(): merged = lax.all_to_all(merged, 'far', 0, 0)  71.4 us
    all_to_all x1, blocking collectives, shards(): partial = lax.all_to_all(partial, BLOCK, 0, 0)  21.1 us
    all_to_all x1, blocking collectives, shards(): finished = lax.all_to_all(finished, BLOCK, 0, 0)  13.7 us
    pallas_call x1, Pallas kernels, shards(): pl.pallas_call(attend_kernel, out_shape=jax.ShapeDtypeStruct((peers, shar...  6.69 us

profile of v1, /device:TPU:40, one launch (start us, length us, event | category | flops | bytes accessed | tf_op | source)
XLA Modules:
  0.0 118.1 jit_solution(11493778524061038642)
XLA Ops:
  0.0 0.6 pad_add_fusion.place
  0.6 6.7 %attend.1 = f32[16,24,128]{2,1,0:T(8,128)} custom-call(s32[2]{0:T(128)} %pad_add_fusion.place, s32[32]{0:T(128)} %batch_row.1, s32[32]{0:T(128)} %lengths.1, s32[32,256]{1,0:T(8,128)} %table.1, bf16[32,32,128]{2,1,0:T(8,128)(2,1)} %queries.1, bf16[8,4,128,128]{3,2,1,0:T(8,128)(2,1)} %k_hbm.1, bf16[8,4,128,128]{3,2,1,0:T(8,128)(2,1)} %v_hbm.1), custom_call_target="tpu_custom_call" | custom-call | tf_op jit(solution)/shard_map/attend/pallas_call | solution.py:200
  7.3 21.1 %all_to_all.15.got = f32[16,24,128]{2,1,0:T(8,128)} all-to-all(f32[16,24,128]{2,1,0:T(8,128)} %attend.1), channel_id=1, replica_groups=mesh['group'=2,'far'=8,'near'=4,'across'=4,'tensor'=2] {'near','across'}, dimensions={0} | all-to-all | bytes 393216 | tf_op jit(solution)/shard_map/all_to_all | solution.py:215
  28.4 2.0 %merge_slots.1 = bf16[8,80,128]{2,1,0:T(8,128)(2,1)} custom-call(f32[16,24,128]{2,1,0:T(8,128)} %all_to_all.15.got), custom_call_target="tpu_custom_call" | custom-call | tf_op jit(solution)/shard_map/merge_slots/pallas_call | solution.py:216
  30.4 71.4 %all_to_all.16.got = bf16[8,80,128]{2,1,0:T(8,128)(2,1)} all-to-all(bf16[8,80,128]{2,1,0:T(8,128)(2,1)} %merge_slots.1), channel_id=1, replica_groups=mesh['group'=2,'far'=8,'near'=4,'across'=4,'tensor'=2] {'far'}, dimensions={0} | all-to-all | bytes 327680 | tf_op jit(solution)/shard_map/all_to_all | solution.py:225
  101.8 1.9 %merge_blocks.1 = bf16[16,64,128]{2,1,0:T(8,128)(2,1)} custom-call(bf16[8,80,128]{2,1,0:T(8,128)(2,1)} %all_to_all.16.got), custom_call_target="tpu_custom_call" | custom-call | tf_op jit(solution)/shard_map/merge_blocks/pallas_call | solution.py:226
  103.7 13.7 %all_to_all.17 = bf16[16,64,128]{2,1,0:T(8,128)(2,1)S(1)} all-to-all(bf16[16,64,128]{2,1,0:T(8,128)(2,1)} %merge_blocks.1), channel_id=1, replica_groups=mesh['group'=2,'far'=8,'near'=4,'across'=4,'tensor'=2] {'near','across'}, dimensions={0} | all-to-all | bytes 524288 | tf_op jit(solution)/shard_map/all_to_all | solution.py:233
  117.3 0.8 copy.9
